TPU v7x, 512 devices: a whole 4x4x16 slice. The times are simulated.
512 devices in a mesh: row: 16 (over z), col: 32 (over x, y, core).
Axes of the slice: x: 4, y: 4, z: 16, core: 2. Of those that a mesh axis runs over, the one named last changes fastest.
Arguments:
- slab_left: bfloat16 [64, 32, 2048, 32], P('row', 'col'), may hold values from -6 to 6
- slab_right: bfloat16 [64, 32, 2048, 32], P('row', 'col'), may hold values from -1 to 1
- slab_ranks: int32 [64, 32], P('row', 'col'), may hold values from 20 to 32
- panel_left: bfloat16 [64, 2048, 32], P('row', 'col'), may hold values from -6 to 6
- panel_right: bfloat16 [64, 2048, 32], P('row', 'col'), may hold values from -0.125 to 0.125
- panel_ranks: int32 [64], P('row'), may hold values from 20 to 32
- inverse_factor: bfloat16 [2048, 2048], P(None, 'col'), may hold values from -2 to 2, as said below
- sketch: bfloat16 [2048, 32], replicated, may hold values from -6 to 6
Outputs:
- new_left: bfloat16 [64, 32, 2048, 32], P('row', 'col')
- new_right: bfloat16 [64, 32, 2048, 32], P('row', 'col')
Inputs may be any that keep to these rules, and one draw needn't show every extreme that they name: `slab_ranks`: number of live columns of a slab tile's factors; columns from that index on are padding. `panel_ranks`: number of live columns of a panel tile's factors; columns from that index on are padding. `inverse_factor`: lower triangular: entries above the diagonal are zero, diagonal entries positive.
All inputs are finite; a program needn't handle non-finite values.
Results may differ from a plain program's by a relative error of at most 0.0073.
Values may be sent and summed in bfloat16 or wider, within the bound.
A program may use at most 64 MiB of HBM per device.

v0:
```python
import math

import jax
import jax.numpy as jnp
from jax import lax
from jax.sharding import PartitionSpec as P

highest = lax.Precision.HIGHEST
stacked_precision = lax.Precision.HIGH
shift_rate = 0.01
tiny_shift = 1e-06
factor_scale = 0.5


def cut_along(x, dim, size):
    before, after = (x.shape[:dim], x.shape[dim + 1 :])
    return jnp.moveaxis(x.reshape(*before, size, -1, *after), dim, 0)


def summed_on_arrival(x, axis, dim):
    blocks = cut_along(x, dim, lax.axis_size(axis))
    arrived = lax.all_to_all(blocks, axis, split_axis=0, concat_axis=0, tiled=True)
    return arrived.sum(axis=0)


def joined_along(blocks, dim):
    blocks = jnp.moveaxis(blocks, 0, dim)
    dims = blocks.shape
    return blocks.reshape(*dims[:dim], dims[dim] * dims[dim + 1], *dims[dim + 2 :])


def copy_for_each(x, axis):
    copies = jnp.broadcast_to(x, (lax.axis_size(axis), *x.shape))
    return lax.all_to_all(copies, axis, split_axis=0, concat_axis=0, tiled=True)


def gathered_copies(x, axis, dim):
    return joined_along(copy_for_each(x, axis), dim)


def side_by_side(arrays, axis, dim, along):
    both = jnp.concatenate(arrays, axis=along)
    whole, at, outs = (gathered_copies(both, axis, dim), 0, [])
    for a in arrays:
        outs.append(lax.slice_in_dim(whole, at, at + a.shape[along], axis=along))
        at += a.shape[along]
    return tuple(outs)


def spread(block, axis, owner):
    block = jnp.where(lax.axis_index(axis) == owner, block, jnp.zeros_like(block))
    return lax.psum(block, axis)


def product(first_matrix, second_matrix):
    return jnp.matmul(first_matrix, second_matrix, precision=highest)


def stacked_product(first_matrix, second_matrix):
    return jnp.matmul(first_matrix, second_matrix, precision=stacked_precision)


def flipped(matrix):
    return jnp.swapaxes(matrix, -1, -2)


def orthonormal(vectors):
    gram_matrix = product(flipped(vectors), vectors)
    shift_value = (
        shift_rate * jnp.trace(gram_matrix, axis1=-2, axis2=-1) / gram_matrix.shape[-1] + tiny_shift
    )
    identity = jnp.eye(gram_matrix.shape[-1], dtype=gram_matrix.dtype)
    lower_factor = jnp.linalg.cholesky(gram_matrix + shift_value[..., None, None] * identity)
    solved_rows = lax.linalg.triangular_solve(
        lower_factor, flipped(vectors), left_side=True, lower=True
    )
    return flipped(solved_rows)


def recompress(slab_factor, masked_right, row_factor, core_block, column_factor, sketch_float):
    target_shape = core_block.shape[:2] + slab_factor.shape[2:]
    column_wide = jnp.broadcast_to(column_factor[None], target_shape)
    row_core = product(row_factor, core_block)
    column_core = product(column_wide, flipped(core_block))
    forward_left = jnp.concatenate([slab_factor.astype(jnp.float32), -row_core], axis=-1)
    forward_right = jnp.concatenate([masked_right.astype(jnp.float32), column_wide], axis=-1)
    backward_left = jnp.concatenate([masked_right.astype(jnp.float32), -column_core], axis=-1)
    backward_right = jnp.concatenate([slab_factor.astype(jnp.float32), row_factor], axis=-1)

    def forward(vectors):
        return stacked_product(forward_left, stacked_product(flipped(forward_right), vectors))

    def backward(vectors):
        return stacked_product(backward_left, stacked_product(flipped(backward_right), vectors))

    basis_now = orthonormal(forward(sketch_float))
    basis_now = orthonormal(forward(backward(basis_now)))
    projected = backward(basis_now)
    factor_size = factor_scale * math.sqrt(slab_factor.shape[-2])
    return (basis_now * factor_size, projected / factor_size)


def shards(
    slab_left, slab_right, slab_ranks, panel_left, panel_right, panel_ranks, inverse_factor, sketch
):
    rows_total = lax.axis_size("row")
    cols_total = lax.axis_size("col")
    my_row = lax.axis_index("row")
    my_col = lax.axis_index("col")
    tile_rows, piece_rows, rank_width = panel_left.shape
    column_tiles = slab_left.shape[1]
    tile_order = inverse_factor.shape[0]
    panel_keep = jnp.arange(rank_width, dtype=jnp.int32)[None, :] < panel_ranks[:, None]
    masked_panel = jnp.where(panel_keep[:, None, :], panel_right, jnp.zeros((), jnp.bfloat16))
    flat_right = jnp.swapaxes(masked_panel, 0, 1).reshape(piece_rows, tile_rows * rank_width)
    flat_left = jnp.swapaxes(panel_left, 0, 1).reshape(piece_rows, tile_rows * rank_width)
    solved_part = summed_on_arrival(
        jnp.dot(inverse_factor, flat_right, preferred_element_type=jnp.float32), "col", 0
    ).astype(jnp.bfloat16)
    full_left, full_solved = side_by_side((flat_left, solved_part), "col", 0, 1)
    full_left = full_left.reshape(tile_order, tile_rows, rank_width)
    full_solved = full_solved.reshape(tile_order, tile_rows, rank_width)
    first_pick = my_col // rows_total
    position = first_pick + 0
    picked_left = lax.dynamic_slice_in_dim(full_left, position, 1, 1)
    picked_solved = lax.dynamic_slice_in_dim(full_solved, position, 1, 1)
    send_left = picked_left.reshape(tile_order, column_tiles * rank_width)
    send_solved = picked_solved.reshape(tile_order, column_tiles * rank_width)
    root_row = my_col % rows_total
    column_left, column_solved = (
        spread(send_left, "row", root_row),
        spread(send_solved, "row", root_row),
    )
    row_factor = jnp.swapaxes(full_left, 0, 1)[:, None]
    row_solved = jnp.swapaxes(full_solved, 0, 1)
    column_factor = jnp.swapaxes(column_left.reshape(tile_order, column_tiles, rank_width), 0, 1)
    column_three = jnp.swapaxes(column_solved.reshape(tile_order, column_tiles, rank_width), 0, 1)
    core_block = jnp.einsum(
        "tbr,sbq->tsrq", row_solved, column_three, preferred_element_type=jnp.float32
    )
    slab_keep = jnp.arange(rank_width, dtype=jnp.int32) < slab_ranks[..., None]
    masked_right = jnp.where(slab_keep[:, :, None, :], slab_right, jnp.zeros((), jnp.bfloat16))
    fresh_left, fresh_right = recompress(
        slab_left, masked_right, row_factor, core_block, column_factor, sketch.astype(jnp.float32)
    )
    row_ids = jnp.arange(tile_rows, dtype=jnp.int32) * rows_total + my_row
    col_ids = jnp.arange(column_tiles, dtype=jnp.int32) * cols_total + my_col
    live_tile = (row_ids[:, None] > col_ids[None, :])[:, :, None, None]
    return (
        jnp.where(live_tile, fresh_left, 0.0).astype(jnp.bfloat16),
        jnp.where(live_tile, fresh_right, 0.0).astype(jnp.bfloat16),
    )


def solution(mesh):
    placed = (
        P("row", "col", None, None),
        P("row", "col", None, None),
        P("row", "col"),
        P("row", "col", None),
        P("row", "col", None),
        P("row"),
        P(None, "col"),
        P(),
    )
    return jax.shard_map(
        shards,
        mesh=mesh,
        in_specs=placed,
        out_specs=(P("row", "col", None, None), P("row", "col", None, None)),
        check_vma=False,
    )
```

profile of v0, /device:TPU:6, one launch (start us, length us, event | category | flops | bytes accessed | tf_op | source)
XLA Modules:
  0.0 282.9 jit_solution(7502040444087477989)
XLA Ops:
  7.2 0.8 iota_compare_fusion.4
  7.9 0.8 broadcast_select_fusion
  8.8 0.3 convolution_bitcast_fusion.1
  9.1 1.3 copy.49
  10.4 9.7 %all-to-all-start = ((f32[32,64,128]{2,1,0:T(8,128)}), f32[32,64,128]{2,1,0:T(8,128)S(1)}, u32[]{:S(2)}, u32[]{:S(2)}) async-start(f32[32,64,128]{2,1,0:T(8,128)} %bitcast.6), calls=%async_computation | async-start | bytes 2097152 | tf_op jit(solution)/shard_map/all_to_all | solution.py:22
  20.3 15.0 %all-to-all-done = f32[32,64,128]{2,1,0:T(8,128)S(1)} async-done(((f32[32,64,128]{2,1,0:T(8,128)}), f32[32,64,128]{2,1,0:T(8,128)S(1)}, u32[]{:S(2)}, u32[]{:S(2)}) %all-to-all-start) | async-done | bytes 1048608 | tf_op jit(solution)/shard_map/all_to_all | solution.py:22
  35.4 1.1 broadcast_in_dim.98
  36.5 5.7 %all-to-all-start.1 = ((bf16[32,64,256]{2,1,0:T(8,128)(2,1)}), bf16[32,64,256]{2,1,0:T(8,128)(2,1)S(1)}, u32[]{:S(2)}, u32[]{:S(2)}) async-start(bf16[32,64,256]{2,1,0:T(8,128)(2,1)} %broadcast_in_dim.98), calls=%async_computation.1 | async-start | bytes 2097152 | tf_op jit(solution)/shard_map/all_to_all | solution.py:34
  42.3 0.6 iota_compare_fusion.1
  42.9 0.1 bitcast_convert_fusion
  43.0 1.2 fusion.35
  44.2 13.4 %all-to-all-done.1 = bf16[32,64,256]{2,1,0:T(8,128)(2,1)S(1)} async-done(((bf16[32,64,256]{2,1,0:T(8,128)(2,1)}), bf16[32,64,256]{2,1,0:T(8,128)(2,1)S(1)}, u32[]{:S(2)}, u32[]{:S(2)}) %all-to-all-start.1) | async-done | bytes 1048608 | tf_op jit(solution)/shard_map/all_to_all | solution.py:34
  57.5 1.0 fusion.66
  58.5 1.2 copy.51
  59.8 1.2 copy.52
  61.0 0.7 select_bitcast_fusion
  61.8 0.5 add_compare_fusion
  62.4 0.6 iota_compare_fusion
  63.0 1.1 convert.1
  64.1 135.1 %all-reduce.3.cloned.1.call-done = (bf16[2048,32]{0,1:T(8,128)(2,1)}, bf16[2048,32]{0,1:T(8,128)(2,1)}) async-done(((bf16[2048,32]{0,1:T(8,128)(2,1)}, bf16[2048,32]{0,1:T(8,128)(2,1)}), (bf16[2048,32]{0,1:T(8,128)(2,1)}, bf16[2048,32]{0,1:T(8,128)(2,1)})) %all-reduce.3.cloned.1.call-update) | async-done | bytes 262160 | tf_op jit(solution)/shard_map/psum | solution.py:52
  199.2 1.4 fusion.38
  200.7 0.6 fusion.2
  201.3 1.7 fusion.1
  202.9 0.1 broadcast_in_dim.101
  203.0 1.0 copy-done.7
  204.0 1.1 fusion.11
  205.1 0.6 fusion.19
  205.8 1.7 select_reduce_fusion.1
  207.5 0.7 multiply_add_fusion.3
  208.2 0.5 copy-done.17
  208.7 0.7 fusion.55
  209.4 0.9 copy.57
  210.3 1.4 fusion.42
  211.7 12.4 %custom-call.8 = f32[4,1,32,32]{3,2,1,0:T(8,128)S(1)} custom-call(f32[4,1,32,32]{3,2,1,0:T(8,128)} %fusion.42), custom_call_target="Cholesky" | custom-call | tf_op jit(solution)/shard_map/jit(cholesky)/cholesky | solution.py:73
  224.1 0.7 fusion.51
  224.8 0.1 compare_reduce_fusion.1
  224.9 0.8 fusion.54
  225.7 9.8 %custom-call.9 = f32[4,1,1,32,32]{3,4,2,1,0:T(8,128)S(1)} custom-call(f32[4,1,1,32,32]{4,3,2,1,0:T(8,128)S(1)} %fusion.54), custom_call_target="InvertDiagBlocksLowerTriangular" | custom-call | tf_op jit(solution)/shard_map/triangular_solve/custom-call.0 | solution.py:74
  235.6 1.1 convolution_bitcast_fusion
  236.6 0.2 copy-done.1
  236.8 1.0 fusion.15
  237.8 0.2 copy-done.5
  238.0 0.6 fusion.22
  238.7 0.6 copy-done.8
  239.3 1.0 fusion.9
  240.3 0.2 copy-done.4
  240.5 0.6 fusion.17
  241.2 1.7 select_reduce_fusion
  242.9 0.7 multiply_add_fusion.2
  243.6 0.5 copy-done.16
  244.1 0.7 fusion.56
  244.8 0.9 copy.63
  245.7 1.4 fusion.40
  247.1 12.4 %custom-call.10 = f32[4,1,32,32]{3,2,1,0:T(8,128)S(1)} custom-call(f32[4,1,32,32]{3,2,1,0:T(8,128)} %fusion.40), custom_call_target="Cholesky" | custom-call | tf_op jit(solution)/shard_map/jit(cholesky)/cholesky | solution.py:73
  259.5 0.7 fusion.46
  260.2 0.1 compare_reduce_fusion
  260.3 0.8 fusion.49
  261.1 9.8 %custom-call.11 = f32[4,1,1,32,32]{3,4,2,1,0:T(8,128)S(1)} custom-call(f32[4,1,1,32,32]{4,3,2,1,0:T(8,128)S(1)} %fusion.49), custom_call_target="InvertDiagBlocksLowerTriangular" | custom-call | tf_op jit(solution)/shard_map/triangular_solve/custom-call.0 | solution.py:74
  271.0 1.1 fusion.24
  272.0 0.2 copy-done.2
  272.2 1.0 fusion.13
  273.2 1.0 fusion.34
  274.2 0.4 copy-done.6
  274.6 1.4 fusion.4
  (40 shorter events, 0.7 us)
Async XLA Ops:
  7.2 1.6 copy-start
  10.4 9.7 %copy-start.14 = (bf16[4,64,32]{1,2,0:T(8,128)(2,1)S(1)}, bf16[4,64,32]{1,2,0:T(8,128)(2,1)}, u32[]{:S(2)}) copy-start(bf16[4,64,32]{1,2,0:T(8,128)(2,1)} %param.14) | copy-start | bytes 49156
  10.4 9.8 %copy-start.18 = (s32[4,1]{0,1:T(1,128)S(1)}, s32[4,1]{0,1:T(1,128)}, u32[]{:S(2)}) copy-start(s32[4,1]{0,1:T(1,128)} %param.13) | copy-start | bytes 52
  10.4 24.9 %all-to-all-start = ((f32[32,64,128]{2,1,0:T(8,128)}), f32[32,64,128]{2,1,0:T(8,128)S(1)}, u32[]{:S(2)}, u32[]{:S(2)}) async-start(f32[32,64,128]{2,1,0:T(8,128)} %bitcast.6), calls=%async_computation | async-start | bytes 2097152 | tf_op jit(solution)/shard_map/all_to_all | solution.py:22
  36.5 6.4 %copy-start.9 = (bf16[4,1,2048,32]{2,3,1,0:T(8,128)(2,1)S(1)}, bf16[4,1,2048,32]{2,3,1,0:T(8,128)(2,1)}, u32[]{:S(2)}) copy-start(bf16[4,1,2048,32]{2,3,1,0:T(8,128)(2,1)} %param.11) | copy-start | bytes 1572868
  36.5 21.0 %all-to-all-start.1 = ((bf16[32,64,256]{2,1,0:T(8,128)(2,1)}), bf16[32,64,256]{2,1,0:T(8,128)(2,1)S(1)}, u32[]{:S(2)}, u32[]{:S(2)}) async-start(bf16[32,64,256]{2,1,0:T(8,128)(2,1)} %broadcast_in_dim.98), calls=%async_computation.1 | async-start | bytes 2097152 | tf_op jit(solution)/shard_map/all_to_all | solution.py:34
  42.2 157.0 %all-reduce.3.cloned.1.call-start = ((), (), s32[]{:S(2)}) async-start(), calls=%async_computation.2 | async-start | bytes 524288 | tf_op jit(solution)/shard_map/psum | solution.py:52
  62.4 143.3 %copy-start.12 = (pred[32,32]{1,0:T(8,128)(4,1)}, pred[32,32]{1,0:T(8,128)(4,1)S(1)}, u32[]{:S(2)}) copy-start(pred[32,32]{1,0:T(8,128)(4,1)S(1)} %copy.55) | copy-start | bytes 3076
  199.2 2.0 copy-start.10
  201.2 3.9 %copy-start.3 = (f32[4,1,2048,32]{2,3,0,1:T(8,128)}, f32[4,1,2048,32]{2,3,0,1:T(8,128)S(1)}, u32[]{:S(2)}) copy-start(f32[4,1,2048,32]{2,3,0,1:T(8,128)S(1)} %fusion.2) | copy-start | bytes 3145732
  201.3 2.8 copy-start.11
  203.0 1.0 copy-start.7
  208.2 0.5 copy-start.17
  235.6 1.3 copy-start.1
  236.8 1.2 copy-start.5
  238.0 1.2 copy-start.8
  239.3 1.2 copy-start.4
  240.5 0.7 copy-start.13
  243.6 0.5 copy-start.16
  270.9 1.3 copy-start.2
  272.2 1.0 copy-start.15
  273.2 1.4 copy-start.6
Sparse Core Ops, SparseCore 0:
  61.9 137.2 all-reduce.2
where the time goes:
time: 284 us; the launch traced here: 283 us
  waiting for transfers between devices  163 us (57%)
  other arithmetic  60.7 us (21%)
  matrix products  16.9 us (6%)
  starting transfers between devices  15.5 us (5%)
  between operations  14.3 us (5%)
  local copies, waits for them, and re-layouts  12.1 us (4%)
    psum x1, waiting for transfers between devices, spread(): return lax.psum(block, axis)  135 us
    another operation x7, other arithmetic, orthonormal(): jnp.linalg.cholesky(gram_matrix + shift_value[..., None, None] * identity)  27.1 us
    another operation x5, other arithmetic, orthonormal(): lax.linalg.triangular_solve(lower_factor, flipped(vectors), left_side=Tru...  21.8 us
    all_to_all x1, waiting for transfers between devices, summed_on_arrival(): lax.all_to_all(blocks, axis, split_axis=0, concat_axis=0, tiled=True)  15 us
    all_to_all x1, waiting for transfers between devices, copy_for_each(): return lax.all_to_all(copies, axis, split_axis=0, concat_axis=0, tiled=True)  13.4 us
    all_to_all x1, starting transfers between devices, summed_on_arrival(): lax.all_to_all(blocks, axis, split_axis=0, concat_axis=0, tiled=True)  9.69 us
    dot_general x8, matrix products, stacked_product(): return jnp.matmul(first_matrix, second_matrix, precision=stacked_precision)  7.43 us
    all_to_all x1, starting transfers between devices, copy_for_each(): return lax.all_to_all(copies, axis, split_axis=0, concat_axis=0, tiled=True)  5.74 us
  transfers between devices with their start and end apart: 3, of which 3 were waited for; matrix products, arithmetic and copies ran while one was open for 2% of the time, Pallas kernels for 0%

commit v1 on v0

v1 whole, which is shorter than its diff:
```python
import functools
import math

import jax
import jax.numpy as jnp
from jax import lax
from jax.experimental import pallas as pl
from jax.experimental.pallas import tpu as pltpu
from jax.sharding import PartitionSpec as P

MESH = pl.DeviceIdType.MESH
HIGHEST = lax.Precision.HIGHEST
f32 = jnp.float32
bf16 = jnp.bfloat16
shift_rate = 0.01
tiny_shift = 1e-06
factor_scale = 0.5
RANK = 32
TILES = 4
ORDER = (0, 2, 1, 3)


def exchange_kernel(
    rows, cols,
    ranks_ref, left_ref, right_ref, inverse_ref,
    full_left, full_solved, column_left, column_solved,
    half_in, masked, partial, arrived, total, left_block, solved_block, left_column, solved_column,
    half_send, half_recv, part_send, part_recv, left_send, left_recv, solved_send, solved_recv,
    zl_send, zl_recv, zs_send, zs_recv, al_send, al_recv, as_send, as_recv,
):
    row, col = lax.axis_index("row"), lax.axis_index("col")
    chips = cols // 2
    chip, core = col // 2, lax.rem(col, 2)
    partner = col + 1 - 2 * core

    def plane(d):
        return lax.rem(col + d, cols)

    def line(d):
        return lax.rem(row + d, rows)

    def each(lo, hi, body):
        def step(d, carry):
            body(d)
            return carry

        lax.fori_loop(lo, hi, step, 0)

    def copy(src, dst, send, recv, where):
        return pltpu.make_async_remote_copy(
            src_ref=src, dst_ref=dst, send_sem=send, recv_sem=recv,
            device_id=where, device_id_type=MESH,
        )

    barrier = pltpu.get_barrier_semaphore()
    each(1, rows, lambda d: pl.semaphore_signal(
        barrier, inc=1, device_id=(line(d), col), device_id_type=MESH))
    each(1, cols, lambda d: pl.semaphore_signal(
        barrier, inc=1, device_id=(row, plane(d)), device_id_type=MESH))

    index = lax.broadcasted_iota(jnp.int32, (RANK, 1), 0)
    for place, tile in enumerate(ORDER):
        keep = index < ranks_ref[tile]
        masked[place * RANK:(place + 1) * RANK, :] = jnp.where(
            keep, right_ref[tile].astype(f32), 0.0).astype(bf16)
    partial[...] = jnp.dot(masked[...], inverse_ref[...], preferred_element_type=f32)

    pl.semaphore_wait(barrier, rows + cols - 2)

    halves = [
        copy(left_ref.at[1 - core + 2 * k], half_in.at[k], half_send.at[k], half_recv.at[k],
             (row, partner))
        for k in range(2)
    ]
    for h in halves:
        h.start()

    own_rows = pl.ds(pl.multiple_of(core * 64, 64), 64)
    own_lanes = pl.ds(pl.multiple_of(chip * 128, 128), 128)

    def part_copy(d):
        there = plane(d)
        src = partial.at[
            pl.ds(pl.multiple_of(lax.rem(there, 2) * 64, 64), 64),
            pl.ds(pl.multiple_of((there // 2) * 128, 128), 128),
        ]
        return copy(src, arrived.at[d], part_send.at[d], part_recv.at[d], (row, there))

    def sends_part(d, act):
        @pl.when(plane(d) // 2 >= chip)
        def _():
            act(d)

    def takes_part(d, act):
        @pl.when(lax.rem(col + cols - d, cols) // 2 <= chip)
        def _():
            act(d)

    def gather_copy(block, full, send, recv, d):
        return copy(block, full.at[own_rows, own_lanes], send.at[d], recv.at[d], (row, plane(d)))

    def line_copy(block, column, send, recv, d):
        return copy(block.at[0:RANK], column.at[d], send.at[d], recv.at[d], (line(d), col))

    def left_copy(d):
        return gather_copy(left_block, full_left, left_send, left_recv, d)

    def solved_copy(d):
        return gather_copy(solved_block, full_solved, solved_send, solved_recv, d)

    def zl_copy(d):
        return line_copy(left_block, left_column, zl_send, zl_recv, d)

    def zs_copy(d):
        return line_copy(solved_block, solved_column, zs_send, zs_recv, d)

    each(1, cols, lambda d: sends_part(d, lambda d: part_copy(d).start()))

    for h in halves:
        h.wait_recv()
    own = jnp.concatenate([left_ref[core], left_ref[2 + core]], axis=0).astype(f32)
    other = jnp.concatenate([half_in[0], half_in[1]], axis=0).astype(f32)
    block = jnp.where(
        core == 0, jnp.concatenate([own, other], axis=1), jnp.concatenate([other, own], axis=1)
    ).astype(bf16)
    left_block[...] = block
    full_left[own_rows, own_lanes] = block
    left_column[0] = block[0:RANK]
    each(1, rows, lambda d: zl_copy(d).start())
    each(1, cols, lambda d: left_copy(d).start())

    total[...] = partial[own_rows, own_lanes]

    def add_part(d):
        part_copy(d).wait_recv()
        total[...] += arrived[d]

    each(1, cols, lambda d: takes_part(d, add_part))
    block = total[...].astype(bf16)
    solved_block[...] = block
    full_solved[own_rows, own_lanes] = block
    solved_column[0] = block[0:RANK]
    each(1, rows, lambda d: zs_copy(d).start())
    each(1, cols, lambda d: solved_copy(d).start())

    def column_copy(column, out, send, recv, d):
        there = lax.rem(row + rows - d, rows) + rows * core
        return there, copy(
            column.at[d], out.at[:, own_lanes], send.at[d], recv.at[chip], (row, there))

    def send_columns(column, out, send, recv):
        def one(d):
            there, c = column_copy(column, out, send, recv, d)

            @pl.when(there != col)
            def _():
                c.start()

            @pl.when(there == col)
            def _():
                out[:, own_lanes] = column[d]

        each(0, rows, one)

    def sent_columns(column, out, send, recv):
        def one(d):
            there, c = column_copy(column, out, send, recv, d)

            @pl.when(there != col)
            def _():
                c.wait_send()

        each(0, rows, one)

    def take_columns(column, out, send, recv):
        def one(x):
            lanes = pl.ds(pl.multiple_of(x * 128, 128), 128)

            @pl.when(2 * x + col // rows != col)
            def _():
                copy(column.at[0], out.at[:, lanes], send.at[0], recv.at[x],
                     (row, partner)).wait_recv()

        each(0, chips, one)

    each(1, rows, lambda d: zl_copy(d).wait_recv())
    send_columns(left_column, column_left, al_send, al_recv)
    each(1, rows, lambda d: zs_copy(d).wait_recv())
    send_columns(solved_column, column_solved, as_send, as_recv)

    each(1, cols, lambda d: left_copy(d).wait_recv())
    each(1, cols, lambda d: solved_copy(d).wait_recv())
    take_columns(left_column, column_left, al_send, al_recv)
    take_columns(solved_column, column_solved, as_send, as_recv)

    for h in halves:
        h.wait_send()
    each(1, cols, lambda d: sends_part(d, lambda d: part_copy(d).wait_send()))
    each(1, cols, lambda d: left_copy(d).wait_send())
    each(1, cols, lambda d: solved_copy(d).wait_send())
    each(1, rows, lambda d: zl_copy(d).wait_send())
    each(1, rows, lambda d: zs_copy(d).wait_send())
    sent_columns(left_column, column_left, al_send, al_recv)
    sent_columns(solved_column, column_solved, as_send, as_recv)


def exchange(rows, cols, ranks, left, right, inverse):
    size = inverse.shape[1]
    vmem = pl.BlockSpec(memory_space=pltpu.VMEM)
    dma = pltpu.SemaphoreType.DMA
    wide = TILES * RANK
    sems = [2, 2] + [cols] * 6 + [rows] * 8
    return pl.pallas_call(
        functools.partial(exchange_kernel, rows, cols),
        out_shape=(
            jax.ShapeDtypeStruct((wide, size), bf16),
            jax.ShapeDtypeStruct((wide, size), bf16),
            jax.ShapeDtypeStruct((RANK, size), bf16),
            jax.ShapeDtypeStruct((RANK, size), bf16),
        ),
        in_specs=[pl.BlockSpec(memory_space=pltpu.SMEM), vmem, vmem, vmem],
        out_specs=(vmem, vmem, vmem, vmem),
        scratch_shapes=[
            pltpu.VMEM((2, RANK, 64), bf16),
            pltpu.VMEM((wide, 64), bf16),
            pltpu.VMEM((wide, size), f32),
            pltpu.VMEM((cols, 64, 128), f32),
            pltpu.VMEM((64, 128), f32),
            pltpu.VMEM((64, 128), bf16),
            pltpu.VMEM((64, 128), bf16),
            pltpu.VMEM((rows, RANK, 128), bf16),
            pltpu.VMEM((rows, RANK, 128), bf16),
        ] + [dma((n,)) for n in sems],
        compiler_params=pltpu.CompilerParams(collective_id=0, has_side_effects=True),
        name="exchange",
    )(ranks, left, right, inverse)


def product(a, b, contract=((1,), (0,))):
    return lax.dot_general(a, b, (contract, ((), ())), precision=HIGHEST,
                           preferred_element_type=f32)


def gram(a, b):
    return lax.dot_general(a, b, (((1,), (1,)), ((), ())), preferred_element_type=f32)


NT = ((1,), (1,))
TN = ((0,), (0,))


def inverse_root(matrix):
    wide = TILES * RANK
    lane = lax.broadcasted_iota(jnp.int32, (RANK, wide), 1)
    sub = lax.broadcasted_iota(jnp.int32, (RANK, wide), 0)
    group = (lane // RANK) * RANK
    eye = jnp.where(lane - group == sub, 1.0, 0.0).astype(f32)
    g = matrix[0:RANK]
    for t in range(1, TILES):
        g = g + matrix[t * RANK:(t + 1) * RANK]
    diagonal = jnp.sum(g * eye, axis=0, keepdims=True)
    same = jnp.where(
        lax.broadcasted_iota(jnp.int32, (wide, wide), 0) // RANK
        == lax.broadcasted_iota(jnp.int32, (wide, wide), 1) // RANK, 1.0, 0.0).astype(f32)
    trace = product(diagonal, same)
    g = g + (shift_rate * trace / RANK + tiny_shift) * eye
    e = eye
    pivots = jnp.zeros((RANK, wide), f32)
    for k in range(RANK):
        column = jnp.take_along_axis(g, group + k, axis=1, mode="promise_in_bounds")
        pivot = column[k:k + 1]
        pivots = jnp.where(sub == k, pivot, pivots)
        if k < RANK - 1:
            m = jnp.where(sub > k, column / pivot, 0.0)
            g = g - m * g[k:k + 1]
            e = e - m * e[k:k + 1]
    compact = e * lax.rsqrt(pivots)
    return jnp.concatenate([compact] * TILES, axis=0) * same


def split(x):
    high = x.astype(bf16)
    return high, (x - high.astype(f32)).astype(bf16)


def recompress_kernel(
    ranks_ref, live_ref, slab_left, slab_right, left_ref, solved_ref, column_left, column_solved,
    sketch_ref, new_left, new_right, left_in, right_in,
):
    wide = TILES * RANK
    size = sketch_ref.shape[1]
    index = lax.broadcasted_iota(jnp.int32, (RANK, 1), 0)
    for place, tile in enumerate(ORDER):
        keep = index < ranks_ref[tile, 0]
        at = slice(place * RANK, (place + 1) * RANK)
        left_in[at, :] = slab_left[tile, 0]
        right_in[at, :] = jnp.where(keep, slab_right[tile, 0].astype(f32), 0.0).astype(bf16)

    def square(n):
        a = lax.broadcasted_iota(jnp.int32, (n, n), 0)
        b = lax.broadcasted_iota(jnp.int32, (n, n), 1)
        return jnp.where((a % wide) // RANK == (b % wide) // RANK, 1.0, 0.0).astype(f32)

    same = square(wide)

    u, v, p = left_in[...], right_in[...], left_ref[...]
    pc, sk = column_left[...], sketch_ref[...]
    core = gram(solved_ref[...], column_solved[...])
    up = gram(u, p) * same
    left_gram = jnp.concatenate([
        jnp.concatenate([gram(u, u) * same, up], axis=1),
        jnp.concatenate([up.T, gram(p, p) * same], axis=1),
    ], axis=0)
    v_v, v_pc, pc_pc = gram(v, v), gram(v, pc), gram(pc, pc)
    v_s, pc_s = gram(v, sk), gram(pc, sk)

    def blocks(x):
        return jnp.concatenate([x] * TILES, axis=1) * same

    cross = product(v_pc, core, NT) * -same
    right_gram = jnp.concatenate([
        jnp.concatenate([v_v * same, cross], axis=1),
        jnp.concatenate([cross.T, product(product(core, pc_pc), core, NT) * same], axis=1),
    ], axis=0)
    x0 = jnp.concatenate([blocks(v_s), blocks(-product(core, pc_s))], axis=0)
    y0 = product(left_gram, x0)
    root0 = inverse_root(product(x0, y0, TN))
    x1 = product(right_gram, product(y0, root0, NT))
    y1 = product(left_gram, x1)
    root1 = inverse_root(product(x1, y1, TN))
    z1 = product(x1, root1, NT)
    w1 = product(y1, root1, NT)
    scale = factor_scale * math.sqrt(size)
    w_low = -product(core, w1[wide:], TN)
    zl = z1 * scale
    w_top = w1[:wide] * (1.0 / scale)
    w_low = w_low * (1.0 / scale)
    zu = jnp.concatenate(split(zl[:wide]), axis=1)
    zp = jnp.concatenate(split(zl[wide:]), axis=1)
    wv = jnp.concatenate(split(w_top), axis=1)
    wc = jnp.concatenate(split(w_low), axis=1)

    def tn(a, b):
        return lax.dot_general(a, b, (TN, ((), ())), preferred_element_type=f32)

    chunk = min(512, size)
    for at in range(0, size, chunk):
        lanes = slice(at, at + chunk)
        q = tn(zu, left_in[:, lanes]) + tn(zp, left_ref[:, lanes])
        r = tn(wv, right_in[:, lanes]) + tn(wc, column_left[:, lanes])
        q = (q[:wide] + q[wide:]).astype(bf16)
        r = (r[:wide] + r[wide:]).astype(bf16)
        for place, tile in enumerate(ORDER):
            rows = slice(place * RANK, (place + 1) * RANK)
            live = live_ref[tile] > 0
            zero = jnp.zeros((RANK, chunk), f32)
            new_left[tile, 0, :, lanes] = jnp.where(live, q[rows].astype(f32), zero).astype(bf16)
            new_right[tile, 0, :, lanes] = jnp.where(live, r[rows].astype(f32), zero).astype(bf16)


def recompress(ranks, live, slab_left, slab_right, left, solved, column_left, column_solved, sketch):
    vmem = pl.BlockSpec(memory_space=pltpu.VMEM)
    smem = pl.BlockSpec(memory_space=pltpu.SMEM)
    wide, size = left.shape
    out = jax.ShapeDtypeStruct(slab_left.shape, bf16)
    return pl.pallas_call(
        recompress_kernel,
        out_shape=(out, out),
        in_specs=[smem, smem] + [vmem] * 7,
        out_specs=(vmem, vmem),
        scratch_shapes=[pltpu.VMEM((wide, size), bf16), pltpu.VMEM((wide, size), bf16)],
        name="recompress",
    )(ranks, live, slab_left, slab_right, left, solved, column_left, column_solved, sketch)


def shards(
    slab_left, slab_right, slab_ranks, panel_left, panel_right, panel_ranks, inverse_factor, sketch
):
    rows, cols = lax.axis_size("row"), lax.axis_size("col")

    def flip(x):
        return jnp.swapaxes(x, -1, -2)

    left, solved, column_left, column_solved = exchange(
        rows, cols, panel_ranks, flip(panel_left), flip(panel_right), flip(inverse_factor))
    ids = jnp.arange(TILES, dtype=jnp.int32) * rows + lax.axis_index("row")
    live = (ids > lax.axis_index("col")).astype(jnp.int32)
    new_left, new_right = recompress(
        slab_ranks, live, flip(slab_left), flip(slab_right), left, solved, column_left,
        column_solved, flip(sketch))
    return flip(new_left), flip(new_right)


def solution(mesh):
    placed = (
        P("row", "col", None, None),
        P("row", "col", None, None),
        P("row", "col"),
        P("row", "col", None),
        P("row", "col", None),
        P("row"),
        P(None, "col"),
        P(),
    )
    return jax.shard_map(
        shards,
        mesh=mesh,
        in_specs=placed,
        out_specs=(P("row", "col", None, None), P("row", "col", None, None)),
        check_vma=False,
    )
```

time: 284 us -> 78.9 us (0.28)
  the two profiles are of different devices: /device:TPU:6 before, /device:TPU:1 now
where the time goes in v1:
time: 78.9 us; the launch traced here: 78.8 us
  Pallas kernels  76.2 us (97%)
  local copies, waits for them, and re-layouts  1.33 us (2%)
    pallas_call x1, Pallas kernels, exchange(): pl.pallas_call(functools.partial(exchange_kernel, rows, cols), out_shape=...  62.3 us
    pallas_call x1, Pallas kernels, recompress(): pl.pallas_call(recompress_kernel, out_shape=(out, out), in_specs=[smem, s...  14 us

profile of v1, /device:TPU:1, one launch (start us, length us, event | category | flops | bytes accessed | tf_op | source)
XLA Modules:
  0.0 78.8 jit_solution(13776076243166712460)
XLA Ops:
  0.6 0.5 compare_convert_fusion.live_ref
  1.2 0.0 copy-start
  1.2 0.7 copy-done
  1.8 0.7 copy.10.ranks_ref
  2.5 62.3 %exchange.1 = (bf16[128,2048]{1,0:T(8,128)(2,1)}, bf16[128,2048]{1,0:T(8,128)(2,1)}, bf16[32,2048]{1,0:T(8,128)(2,1)}, bf16[32,2048]{1,0:T(8,128)(2,1)}) custom-call(s32[4]{0:T(128)} %ranks_ref.2, bf16[4,32,64]{2,1,0:T(8,128)(2,1)} %bitcast.12, bf16[4,32,64]{2,1,0:T(8,128)(2,1)} %bitcast.13, bf16[64,2048]{1,0:T(8,128)(2,1)} %bitcast.10), custom_call_target="tpu_custom_call" | custom-call | tf_op jit(solution)/shard_map/exchange/pallas_call | solution.py:213
  64.8 14.0 %recompress.1 = (bf16[4,1,32,2048]{3,2,1,0:T(8,128)(2,1)}, bf16[4,1,32,2048]{3,2,1,0:T(8,128)(2,1)}) custom-call(s32[4,1]{1,0:T(4,128)} %copy.10.ranks_ref, s32[4]{0:T(128)} %compare_convert_fusion.live_ref, bf16[4,1,32,2048]{3,2,1,0:T(8,128)(2,1)} %bitcast.8, bf16[4,1,32,2048]{3,2,1,0:T(8,128)(2,1)} %bitcast.9, ...), custom_call_target="tpu_custom_call" | custom-call | tf_op jit(solution)/shard_map/recompress/pallas_call | solution.py:366
Async XLA Ops:
  1.2 0.7 copy-start

commit v2 on v1

v2 whole, which is shorter than its diff:
```python
import functools
import math

import jax
import jax.numpy as jnp
from jax import lax
from jax.experimental import pallas as pl
from jax.experimental.pallas import tpu as pltpu
from jax.sharding import PartitionSpec as P

MESH = pl.DeviceIdType.MESH
HIGHEST = lax.Precision.HIGHEST
f32 = jnp.float32
bf16 = jnp.bfloat16
shift_rate = 0.01
tiny_shift = 1e-06
factor_scale = 0.5
RANK = 32
TILES = 4
ORDER = (0, 2, 1, 3)


def exchange_kernel(
    rows, cols,
    ranks_hbm, left_hbm, right_hbm, inverse_hbm, tile_ranks_hbm, slab_left, slab_right, sketch_hbm,
    full_left, column_left, rows_left, rows_right, left_gram, right_gram, mixed_gram, core_block,
    ranks_ref, tile_ranks, left_ref, right_ref, inverse_ref, sketch_ref, slab_v, load_sem,
    full_solved, column_solved,
    left_in, right_in, inverse_in, partial, arrived, total,
    left_block, solved_block,
    pair_send, pair_recv, part_send, part_recv, left_send, left_recv, solved_send, solved_recv,
    pass_send, pass_recv,
    cl_send, cl_recv, cs_send, cs_recv,
):
    row, col = lax.axis_index("row"), lax.axis_index("col")
    chips = cols // 2
    chip, core = col // 2, lax.rem(col, 2)
    partner = col + 1 - 2 * core

    def line(d):
        return lax.rem(row + d, rows)

    def each(lo, hi, body):
        def step(d, carry):
            body(d)
            return carry

        lax.fori_loop(lo, hi, step, 0)

    def copy(src, dst, send, recv, where):
        return pltpu.make_async_remote_copy(
            src_ref=src, dst_ref=dst, send_sem=send, recv_sem=recv,
            device_id=where, device_id_type=MESH,
        )

    barrier = pltpu.get_barrier_semaphore()
    root, root_core = lax.rem(col, rows), col // rows
    keeps = jnp.logical_and(row == root, core == root_core)

    def hello(to_row, to_col):
        pl.semaphore_signal(barrier, inc=1, device_id=(to_row, to_col), device_id_type=MESH)

    def greet_source(x):
        @pl.when(jnp.logical_not(jnp.logical_and(keeps, x == chip)))
        def _():
            hello(root, 2 * x + root_core)

    each(0, chips, greet_source)
    each(1, chips, lambda d: hello(row, 2 * lax.rem(chip + d, chips) + core))
    hello(row, partner)

    loads = [
        pltpu.make_async_copy(src, dst, load_sem.at[n])
        for n, (src, dst) in enumerate((
            (ranks_hbm, ranks_ref), (right_hbm, right_ref), (inverse_hbm, inverse_ref),
            (left_hbm, left_ref), (tile_ranks_hbm, tile_ranks), (sketch_hbm, sketch_ref),
            (slab_right, slab_v),
        ))
    ] + [
        pltpu.make_async_copy(
            slab_left.at[tile, 0], rows_left.at[place * RANK:(place + 1) * RANK],
            load_sem.at[7 + place])
        for place, tile in enumerate(ORDER)
    ]
    for c in loads:
        c.start()
    for c in loads[:4]:
        c.wait()

    index = lax.broadcasted_iota(jnp.int32, (RANK, 1), 0)

    def masked(first, second):
        return jnp.concatenate([
            jnp.where(index < ranks_ref[core + 2 * k], x.astype(f32), 0.0)
            for k, x in enumerate((first, second))
        ], axis=0).astype(bf16)

    partial[...] = jnp.dot(
        masked(right_ref[core], right_ref[2 + core]), inverse_ref[...],
        preferred_element_type=f32)

    pl.semaphore_wait(barrier, rows + chips - jnp.where(keeps, 1, 0))

    ends = (row, partner)
    pairs = [copy(inverse_ref, inverse_in, pair_send.at[0], pair_recv.at[0], ends)]
    for k in range(2):
        pairs.append(copy(
            right_ref.at[1 - core + 2 * k], right_in.at[k],
            pair_send.at[1 + k], pair_recv.at[1 + k], ends))
    for k in range(2):
        pairs.append(copy(
            left_ref.at[1 - core + 2 * k], left_in.at[k],
            pair_send.at[3 + k], pair_recv.at[3 + k], ends))
    for c in pairs[1:] + pairs[:1]:
        c.start()

    own_rows = pl.ds(pl.multiple_of(core * 64, 64), 64)

    def lanes_of(x):
        return pl.ds(pl.multiple_of(x * 128, 128), 128)

    own_lanes = lanes_of(chip)

    def there(d):
        return lax.rem(chip + d, chips)

    def part_copy(d):
        return copy(partial.at[:, lanes_of(there(d))], arrived.at[d], part_send.at[d],
                    part_recv.at[d], (row, 2 * there(d) + core))

    def sends_part(d, act):
        @pl.when(there(d) > chip)
        def _():
            act(d)

    def takes_part(d, act):
        @pl.when(lax.rem(chip + chips - d, chips) < chip)
        def _():
            act(d)

    def gather_copy(block, full, send, recv, d):
        return copy(block, full.at[own_rows, own_lanes], send.at[d], recv.at[d],
                    (row, 2 * there(d) + core))

    target = row + rows * core

    def column_copy(block, out, send, recv, d):
        return copy(block.at[0:RANK], out.at[:, own_lanes], send.at[d], recv.at[chip],
                    (line(d), target))

    def sends_column(d, act):
        @pl.when(jnp.logical_not(jnp.logical_and(keeps, d == 0)))
        def _():
            act(d)

    def send_columns(block, out, send, recv):
        each(0, rows, lambda d: sends_column(
            d, lambda d: column_copy(block, out, send, recv, d).start()))

        @pl.when(keeps)
        def _():
            out[:, own_lanes] = block[0:RANK]

    def sent_columns(block, out, send, recv):
        each(0, rows, lambda d: sends_column(
            d, lambda d: column_copy(block, out, send, recv, d).wait_send()))

    def take_columns(block, out, send, recv):
        def one(x):
            @pl.when(jnp.logical_not(jnp.logical_and(keeps, x == chip)))
            def _():
                copy(block.at[0:RANK], out.at[:, lanes_of(x)], send.at[0], recv.at[x],
                     ends).wait_recv()

        each(0, chips, one)

    def left_copy(d):
        return gather_copy(left_block, full_left, left_send, left_recv, d)

    def solved_copy(d):
        return gather_copy(solved_block, full_solved, solved_send, solved_recv, d)

    for c in pairs[1:]:
        c.wait_recv()
    own = jnp.concatenate([left_ref[core], left_ref[2 + core]], axis=0).astype(f32)
    other = jnp.concatenate([left_in[0], left_in[1]], axis=0).astype(f32)
    block = jnp.where(
        core == 0, jnp.concatenate([own, other], axis=1), jnp.concatenate([other, own], axis=1)
    ).astype(bf16)
    left_block[...] = block
    full_left[own_rows, own_lanes] = block
    send_columns(left_block, column_left, cl_send, cl_recv)
    pairs[0].wait_recv()
    partial[...] += jnp.dot(
        masked(right_in[0], right_in[1]), inverse_in[...], preferred_element_type=f32)
    each(1, chips, lambda d: sends_part(d, lambda d: part_copy(d).start()))

    for c in loads[4:]:
        c.wait()
    for place, tile in enumerate(ORDER):
        keep = index < tile_ranks[tile]
        rows_right[place * RANK:(place + 1) * RANK, :] = jnp.where(
            keep, slab_v[tile, 0].astype(f32), 0.0).astype(bf16)
    wide = TILES * RANK
    same = same_tile()
    left_gram[0:wide, 0:wide] = gram(rows_left[...], rows_left[...]) * same
    right_gram[...] = gram(rows_right[...], rows_right[...]) * same
    mixed_gram[0:wide, 0:RANK] = gram(rows_right[...], sketch_ref[...])

    total[...] = partial[:, own_lanes]

    def add_part(d):
        part_copy(d).wait_recv()
        total[...] += arrived[d]

    each(1, chips, lambda d: takes_part(d, add_part))
    block = total[...].astype(bf16)
    solved_block[...] = block
    full_solved[own_rows, own_lanes] = block
    send_columns(solved_block, column_solved, cs_send, cs_recv)
    each(1, chips, lambda d: solved_copy(d).start())
    each(1, chips, lambda d: left_copy(d).start())

    def pass_on(full, k):
        part = full.at[own_rows, :]
        return copy(part, part, pass_send.at[k], pass_recv.at[k], ends)

    each(1, chips, lambda d: solved_copy(d).wait_recv())
    pass_on(full_solved, 0).start()
    each(1, chips, lambda d: left_copy(d).wait_recv())
    pass_on(full_left, 1).start()

    take_columns(left_block, column_left, cl_send, cl_recv)
    low = slice(wide, wide + RANK)
    mixed_gram[low, 0:RANK] = gram(column_left[...], sketch_ref[...])
    mixed_gram[0:wide, RANK:2 * RANK] = gram(rows_right[...], column_left[...])
    mixed_gram[low, RANK:2 * RANK] = gram(column_left[...], column_left[...])
    pass_on(full_left, 1).wait_recv()
    left_gram[0:wide, wide:2 * wide] = gram(rows_left[...], full_left[...]) * same
    left_gram[wide:2 * wide, 0:wide] = gram(full_left[...], rows_left[...]) * same
    left_gram[wide:2 * wide, wide:2 * wide] = gram(full_left[...], full_left[...]) * same
    pass_on(full_solved, 0).wait_recv()
    take_columns(solved_block, column_solved, cs_send, cs_recv)
    core_block[...] = gram(full_solved[...], column_solved[...])

    for c in pairs:
        c.wait_send()
    each(1, chips, lambda d: sends_part(d, lambda d: part_copy(d).wait_send()))
    each(1, chips, lambda d: left_copy(d).wait_send())
    each(1, chips, lambda d: solved_copy(d).wait_send())
    sent_columns(left_block, column_left, cl_send, cl_recv)
    sent_columns(solved_block, column_solved, cs_send, cs_recv)
    pass_on(full_solved, 0).wait_send()
    pass_on(full_left, 1).wait_send()


def exchange(rows, cols, ranks, left, right, inverse, tile_ranks, slab_left, slab_right, sketch):
    size = inverse.shape[1]
    vmem = pl.BlockSpec(memory_space=pltpu.VMEM)
    hbm = pl.BlockSpec(memory_space=pltpu.HBM)
    dma = pltpu.SemaphoreType.DMA
    wide = TILES * RANK
    sems = [5, 5] + [cols // 2] * 6 + [2, 2] + [rows, cols // 2] * 2
    shape = jax.ShapeDtypeStruct
    return pl.pallas_call(
        functools.partial(exchange_kernel, rows, cols),
        out_shape=(
            shape((wide, size), bf16),
            shape((RANK, size), bf16),
            shape((wide, size), bf16),
            shape((wide, size), bf16),
            shape((2 * wide, 2 * wide), f32),
            shape((wide, wide), f32),
            shape((wide + RANK, 2 * RANK), f32),
            shape((wide, RANK), f32),
        ),
        in_specs=[hbm] * 8,
        out_specs=(vmem,) * 8,
        scratch_shapes=[
            pltpu.SMEM(ranks.shape, jnp.int32),
            pltpu.SMEM(tile_ranks.shape, jnp.int32),
            pltpu.VMEM(left.shape, bf16),
            pltpu.VMEM(right.shape, bf16),
            pltpu.VMEM(inverse.shape, bf16),
            pltpu.VMEM(sketch.shape, bf16),
            pltpu.VMEM(slab_right.shape, bf16),
            dma((11,)),
            pltpu.VMEM((wide, size), bf16),
            pltpu.VMEM((RANK, size), bf16),
            pltpu.VMEM((2, RANK, 64), bf16),
            pltpu.VMEM((2, RANK, 64), bf16),
            pltpu.VMEM((64, size), bf16),
            pltpu.VMEM((64, size), f32),
            pltpu.VMEM((cols // 2, 64, 128), f32),
            pltpu.VMEM((64, 128), f32),
            pltpu.VMEM((64, 128), bf16),
            pltpu.VMEM((64, 128), bf16),
        ] + [dma((n,)) for n in sems],
        compiler_params=pltpu.CompilerParams(
            collective_id=0, has_side_effects=True),
        name="exchange",
    )(ranks, left, right, inverse, tile_ranks, slab_left, slab_right, sketch)


def same_tile():
    wide = TILES * RANK
    a = lax.broadcasted_iota(jnp.int32, (wide, wide), 0)
    b = lax.broadcasted_iota(jnp.int32, (wide, wide), 1)
    return jnp.where(a // RANK == b // RANK, 1.0, 0.0).astype(f32)


def product(a, b, contract=((1,), (0,))):
    return lax.dot_general(a, b, (contract, ((), ())), precision=HIGHEST,
                           preferred_element_type=f32)


def gram(a, b):
    return lax.dot_general(a, b, (((1,), (1,)), ((), ())), preferred_element_type=f32)


NT = ((1,), (1,))
TN = ((0,), (0,))


def inverse_root(matrix):
    wide = TILES * RANK
    lane = lax.broadcasted_iota(jnp.int32, (RANK, wide), 1)
    sub = lax.broadcasted_iota(jnp.int32, (RANK, wide), 0)
    group = (lane // RANK) * RANK
    eye = jnp.where(lane - group == sub, 1.0, 0.0).astype(f32)
    g = matrix[0:RANK]
    for t in range(1, TILES):
        g = g + matrix[t * RANK:(t + 1) * RANK]
    diagonal = jnp.sum(g * eye, axis=0, keepdims=True)
    same = same_tile()
    trace = product(diagonal, same)
    g = g + (shift_rate * trace / RANK + tiny_shift) * eye
    e = eye
    pivots = jnp.zeros((RANK, wide), f32)

    def spread(k):
        return jnp.take_along_axis(g, group + k, axis=1, mode="promise_in_bounds")

    column = spread(0)
    for k in range(RANK):
        pivot = column[k:k + 1]
        pivots = jnp.where(sub == k, pivot, pivots)
        if k < RANK - 1:
            m = jnp.where(sub > k, column * (1.0 / pivot), 0.0)
            column = spread(k + 1) - m * column[k + 1:k + 2]
            g = g - m * g[k:k + 1]
            e = e - m * e[k:k + 1]
    compact = e * lax.rsqrt(pivots)
    return jnp.concatenate([compact] * TILES, axis=0) * same


def split(x):
    high = x.astype(bf16)
    return high, (x - high.astype(f32)).astype(bf16)


def recompress_kernel(
    left_ref, column_left, left_in, right_in, left_gram_ref, right_ref, mixed, core_ref,
    new_left, new_right,
):
    wide = TILES * RANK
    size = left_ref.shape[1]
    same = same_tile()
    core, left_gram = core_ref[...], left_gram_ref[...]
    v_s, v_pc = mixed[0:wide, 0:RANK], mixed[0:wide, RANK:2 * RANK]
    pc_s, pc_pc = mixed[wide:wide + RANK, 0:RANK], mixed[wide:wide + RANK, RANK:2 * RANK]

    def blocks(x):
        return jnp.concatenate([x] * TILES, axis=1) * same

    cross = product(v_pc, core, NT) * -same
    right_gram = jnp.concatenate([
        jnp.concatenate([right_ref[...], cross], axis=1),
        jnp.concatenate([cross.T, product(product(core, pc_pc), core, NT) * same], axis=1),
    ], axis=0)
    x0 = jnp.concatenate([blocks(v_s), blocks(-product(core, pc_s))], axis=0)
    y0 = product(left_gram, x0)
    root0 = inverse_root(product(x0, y0, TN))
    x1 = product(right_gram, product(y0, root0, NT))
    y1 = product(left_gram, x1)
    root1 = inverse_root(product(x1, y1, TN))
    z1 = product(x1, root1, NT)
    w1 = product(y1, root1, NT)
    scale = factor_scale * math.sqrt(size)
    w_low = -product(core, w1[wide:], TN)
    zl = z1 * scale
    w_top = w1[:wide] * (1.0 / scale)
    w_low = w_low * (1.0 / scale)
    zu = jnp.concatenate(split(zl[:wide]), axis=1)
    zp = jnp.concatenate(split(zl[wide:]), axis=1)
    wv = jnp.concatenate(split(w_top), axis=1)
    wc = jnp.concatenate(split(w_low), axis=1)

    def tn(a, b):
        return lax.dot_general(a, b, (TN, ((), ())), preferred_element_type=f32)

    chunk = min(512, size)
    for at in range(0, size, chunk):
        lanes = slice(at, at + chunk)
        q = tn(zu, left_in[:, lanes]) + tn(zp, left_ref[:, lanes])
        r = tn(wv, right_in[:, lanes]) + tn(wc, column_left[:, lanes])
        q = (q[:wide] + q[wide:]).astype(bf16)
        r = (r[:wide] + r[wide:]).astype(bf16)
        for place, tile in enumerate(ORDER):
            rows = slice(place * RANK, (place + 1) * RANK)
            live = tile * lax.axis_size("row") + lax.axis_index("row") > lax.axis_index("col")
            zero = jnp.zeros((RANK, chunk), f32)
            new_left[tile, 0, :, lanes] = jnp.where(live, q[rows].astype(f32), zero).astype(bf16)
            new_right[tile, 0, :, lanes] = jnp.where(live, r[rows].astype(f32), zero).astype(bf16)


def recompress(shape, *parts):
    vmem = pl.BlockSpec(memory_space=pltpu.VMEM)
    out = jax.ShapeDtypeStruct(shape, bf16)
    return pl.pallas_call(
        recompress_kernel,
        out_shape=(out, out),
        in_specs=[vmem] * len(parts),
        out_specs=(vmem, vmem),
        name="recompress",
    )(*parts)


def shards(
    slab_left, slab_right, slab_ranks, panel_left, panel_right, panel_ranks, inverse_factor, sketch
):
    rows, cols = lax.axis_size("row"), lax.axis_size("col")

    def flip(x):
        return jnp.swapaxes(x, -1, -2)

    slab_left, slab_right = flip(slab_left), flip(slab_right)
    parts = exchange(
        rows, cols, panel_ranks, flip(panel_left), flip(panel_right), flip(inverse_factor),
        slab_ranks.reshape(TILES), slab_left, slab_right, flip(sketch))
    new_left, new_right = recompress(slab_left.shape, *parts)
    return flip(new_left), flip(new_right)


def solution(mesh):
    placed = (
        P("row", "col", None, None),
        P("row", "col", None, None),
        P("row", "col"),
        P("row", "col", None),
        P("row", "col", None),
        P("row"),
        P(None, "col"),
        P(),
    )
    return jax.shard_map(
        shards,
        mesh=mesh,
        in_specs=placed,
        out_specs=(P("row", "col", None, None), P("row", "col", None, None)),
        check_vma=False,
    )
```

time: 78.9 us -> 59.2 us (0.75)
  Pallas kernels: 76.2 us -> 58.4 us
  local copies, waits for them, and re-layouts: 1.33 us -> 0 us
    pallas_call x1, Pallas kernels: 62.3 us -> 48.1 us  [exchange(): pl.pallas_call(functools.partial(exchange_kernel, rows, cols), out_shape=...]
    pallas_call x1, Pallas kernels: 14 us -> 10.4 us  [recompress(): pl.pallas_call(recompress_kernel, out_shape=(out, out), in_specs=[vmem] *...]
    unnamed x3 -> x0, local copies, waits for them, and re-layouts: 1.33 us -> none
where the time goes in v2:
time: 59.2 us; the launch traced here: 59.1 us
  Pallas kernels  58.4 us (99%)
  between operations  0.64 us (1%)
    pallas_call x1, Pallas kernels, exchange(): pl.pallas_call(functools.partial(exchange_kernel, rows, cols), out_shape=...  48.1 us
    pallas_call x1, Pallas kernels, recompress(): pl.pallas_call(recompress_kernel, out_shape=(out, out), in_specs=[vmem] *...  10.4 us

profile of v2, /device:TPU:1, one launch (start us, length us, event | category | flops | bytes accessed | tf_op | source)
XLA Modules:
  0.0 59.1 jit_solution(844310613838452778)
XLA Ops:
  0.6 48.1 %exchange.1 = (bf16[128,2048]{1,0:T(8,128)(2,1)}, bf16[32,2048]{1,0:T(8,128)(2,1)}, bf16[128,2048]{1,0:T(8,128)(2,1)}, bf16[128,2048]{1,0:T(8,128)(2,1)}, f32[25...) custom-call(s32[4]{0:T(128)} %ranks_hbm.1, bf16[4,32,64]{2,1,0:T(8,128)(2,1)} %bitcast.13, ...), custom_call_target="tpu_custom_call" | custom-call | tf_op jit(solution)/shard_map/exchange/pallas_call | solution.py:265
  48.7 10.4 %recompress.1 = (bf16[4,1,32,2048]{3,2,1,0:T(8,128)(2,1)}, bf16[4,1,32,2048]{3,2,1,0:T(8,128)(2,1)}) custom-call(bf16[128,2048]{1,0:T(8,128)(2,1)} %get-tuple-element.12.left_ref, bf16[32,2048]{1,0:T(8,128)(2,1)} %get-tuple-element.13.column_left, bf16[128,2048]{1,0:T(8,128)(2,1)} %get-tuple-element.14.left_in, ...), custom_call_target="tpu_custom_call" | custom-call | tf_op jit(solution)/shard_map/recompress/pallas_call | solution.py:420
